TPU v7x, 16 devices: a 4x2x1 block of a 4x4x8 slice. The times are simulated.
16 devices in a mesh: data: 2 (over y, z), expert: 8 (over x, core).
Axes of the slice: x: 4, y: 2, z: 1, core: 2. Of those that a mesh axis runs over, the one named last changes fastest.
The devices are a block of a 4x4x8 slice.
Arguments:
- x_tok: bfloat16 [32768, 2048], P(('data', 'expert')), parts along dimension 0
- topk_idx: int32 [32768, 2], P(('data', 'expert')), parts along dimension 0
- topk_w: float32 [32768, 2], P(('data', 'expert')), parts along dimension 0
- w_up: bfloat16 [8, 2048, 5632], P('expert')
- w_down: bfloat16 [8, 5632, 2048], P('expert')
Outputs:
- output: bfloat16 [32768, 2048], P(('data', 'expert')), parts along dimension 0
There are 2 independent parts. A program takes and returns all parts, laid end to end along the dimension named above; an argument that names none is the same for every part.
All inputs are finite; a program needn't handle non-finite values.
Results may differ from a plain program's by a relative error of at most 0.0013.
Values are sent between devices in bfloat16 or wider.
A program may use at most 768 MiB of HBM per device.

v0:
```python
import functools

import jax
import jax.numpy as jnp
from jax import lax
from jax.experimental import pallas as pl
from jax.experimental.pallas import tpu as pltpu
from jax.sharding import PartitionSpec as P

SLOTS = 448
SUB = 256
SUBS = 7
FF_STEP = 512
RING = 64
MESH = pl.DeviceIdType.MESH


class Way:
    def __init__(self, pieces, lag, group):
        self.pieces, self.lag = pieces, lag
        self.slots = pieces + (group - 2) * lag

    def bind(self, owner, weights, landed, both, out, own_sem, got_sem, send_sem, recv_sem, target):
        self.owner, self.weights, self.landed, self.both, self.out = owner, weights, landed, both, out
        self.own_sem, self.got_sem, self.send_sem, self.recv_sem, self.target = own_sem, got_sem, send_sem, recv_sem, target

    def remote(self, t):
        return pltpu.make_async_remote_copy(
            src_ref=self.out.at[t % 3], dst_ref=self.landed.at[t], send_sem=self.send_sem.at[t % 3],
            recv_sem=self.recv_sem.at[t % RING], device_id={'expert': self.target}, device_id_type=MESH)

    def own(self, t):
        return pltpu.make_async_copy(self.weights.at[t], self.both.at[t % 2, 1], self.own_sem.at[t % 2])

    def got(self, t):
        return pltpu.make_async_copy(self.landed.at[t - self.lag], self.both.at[t % 2, 0], self.got_sem.at[t % 2])

    def load(self, t):
        @pl.when(t < self.pieces)
        def _():
            self.own(t).start()

        @pl.when(t >= self.lag)
        def _():
            self.remote(t - self.lag).wait_recv()
            self.got(t).start()

    def choose(self, t):
        @pl.when(t < self.pieces)
        def _():
            self.own(t).wait()

        @pl.when(t >= self.lag)
        def _():
            self.got(t).wait()

        @pl.when(t >= 3)
        def _():
            self.remote(t - 3).wait_send()

        which = jnp.where(t < self.lag, 1, jnp.where(t < self.pieces, self.owner[0], 0))
        self.out[t % 3] = self.both[t % 2, which]

    def event(self, t):
        @pl.when((t >= 1) & (t <= self.slots))
        def _():
            self.remote(t - 1).start()

        @pl.when(t < self.slots)
        def _():
            self.choose(t)

        @pl.when(t + 1 < self.slots)
        def _():
            self.load(t + 1)

    def finish(self):
        for t in range(self.slots - 3, self.slots):
            self.remote(t).wait_send()
        for t in range(self.slots - self.lag, self.slots):
            self.remote(t).wait_recv()


def ring_ffn_kernel(group, up_way, down_way, owner, x_hbm, up_hbm, down_hbm, up_pieces, down_pieces,
                    o_hbm, up_landed, down_landed,
                    x_buf, acc, up_buf, down_buf, o_buf, x_sem, w_sem, o_sem,
                    up_both, up_out, up_own_sem, up_got_sem, up_send_sem, up_recv_sem,
                    down_both, down_out, down_own_sem, down_got_sem, down_send_sem, down_recv_sem):
    me = lax.axis_index('expert')
    right, left = lax.rem(me + 1, group), lax.rem(me + group - 1, group)
    barrier = pltpu.get_barrier_semaphore()
    for other in (left, right):
        pl.semaphore_signal(barrier, inc=1, device_id={'expert': other}, device_id_type=MESH)
    pl.semaphore_wait(barrier, 2)
    up_way.bind(owner, up_pieces, up_landed, up_both, up_out, up_own_sem, up_got_sem, up_send_sem, up_recv_sem, right)
    down_way.bind(owner, down_pieces, down_landed, down_both, down_out, down_own_sem, down_got_sem, down_send_sem, down_recv_sem, left)

    big = SUB * SUBS
    supers = x_hbm.shape[0] // big
    n_ff = up_hbm.shape[1] // FF_STEP
    steps = supers * n_ff

    def x_copy(p):
        return pltpu.make_async_copy(x_hbm.at[pl.ds(pl.multiple_of(p * big, big), big)], x_buf.at[p % 2], x_sem.at[p % 2])

    def w_copies(s):
        cols = pl.ds(pl.multiple_of((s % n_ff) * FF_STEP, FF_STEP), FF_STEP)
        return (pltpu.make_async_copy(up_hbm.at[:, cols], up_buf.at[s % 2], w_sem.at[0, s % 2]),
                pltpu.make_async_copy(down_hbm.at[cols], down_buf.at[s % 2], w_sem.at[1, s % 2]))

    def o_copy(i):
        return pltpu.make_async_copy(o_buf.at[i % 2], o_hbm.at[pl.ds(pl.multiple_of(i * SUB, SUB), SUB)], o_sem.at[i % 2])

    def compute(e):
        s, sub = e // SUBS, e % SUBS
        p, f = s // n_ff, s % n_ff

        @pl.when((sub == 0) & (f == 0))
        def _():
            x_copy(p).wait()

            @pl.when(p + 1 < supers)
            def _():
                x_copy(p + 1).start()

        @pl.when(sub == 0)
        def _():
            for c in w_copies(s):
                c.wait()

            @pl.when(s + 1 < steps)
            def _():
                for c in w_copies(s + 1):
                    c.start()

        rows = pl.ds(pl.multiple_of(sub * SUB, SUB), SUB)
        h = jnp.dot(x_buf[p % 2, rows, :], up_buf[s % 2], preferred_element_type=jnp.float32)
        h = gelu(h).astype(jnp.bfloat16)
        part = jnp.dot(h, down_buf[s % 2], preferred_element_type=jnp.float32)

        @pl.when(f == 0)
        def _():
            acc[rows, :] = part

        @pl.when((f > 0) & (f < n_ff - 1))
        def _():
            acc[rows, :] += part

        @pl.when(f == n_ff - 1)
        def _():
            i = p * SUBS + sub

            @pl.when(i >= 2)
            def _():
                o_copy(i - 2).wait()
            o_buf[i % 2] = (acc[rows, :] + part).astype(jnp.bfloat16)
            o_copy(i).start()

    x_copy(0).start()
    for c in w_copies(0):
        c.start()
    up_way.load(0)
    down_way.load(0)

    def body(e, carry):
        @pl.when(e <= up_way.slots)
        def _():
            up_way.event(e)

        b = (e // 4) * 3 + e % 4

        @pl.when((e % 4 != 3) & (b <= down_way.slots))
        def _():
            down_way.event(b)

        @pl.when(e < steps * SUBS)
        def _():
            compute(e)
        return carry

    n_events = max(steps * SUBS, up_way.slots + 1, (down_way.slots // 3 + 1) * 4)
    lax.fori_loop(0, n_events, body, 0)
    up_way.finish()
    down_way.finish()
    n_out = supers * SUBS
    o_copy(n_out - 2).wait()
    o_copy(n_out - 1).wait()


def ring_ffn(group, owner, x, up, down):
    n_rows, d_model = x.shape
    d_ff = up.shape[1]
    up_rows, down_rows = 16, 64
    up_way, down_way = Way(d_model // up_rows, 5, group), Way(d_ff // down_rows, 4, group)
    up_pieces = up.reshape(d_model // up_rows, up_rows, d_ff)
    down_pieces = down.reshape(d_ff // down_rows, down_rows, d_model)
    hbm = pl.BlockSpec(memory_space=pl.ANY)
    big = SUB * SUBS
    dma = pltpu.SemaphoreType.DMA

    def ring_scratch(rows, cols):
        return [pltpu.VMEM((2, 2, rows, cols), jnp.bfloat16), pltpu.VMEM((3, rows, cols), jnp.bfloat16),
                dma((2,)), dma((2,)), dma((3,)), dma((RING,))]

    out, up_landed, down_landed = pl.pallas_call(
        functools.partial(ring_ffn_kernel, group, up_way, down_way),
        out_shape=(jax.ShapeDtypeStruct((n_rows, d_model), jnp.bfloat16),
                   jax.ShapeDtypeStruct((up_way.slots, up_rows, d_ff), jnp.bfloat16),
                   jax.ShapeDtypeStruct((down_way.slots, down_rows, d_model), jnp.bfloat16)),
        in_specs=[pl.BlockSpec(memory_space=pltpu.SMEM), hbm, hbm, hbm, hbm, hbm],
        out_specs=(hbm, hbm, hbm),
        scratch_shapes=[
            pltpu.VMEM((2, big, d_model), jnp.bfloat16),
            pltpu.VMEM((big, d_model), jnp.float32),
            pltpu.VMEM((2, d_model, FF_STEP), jnp.bfloat16),
            pltpu.VMEM((2, FF_STEP, d_model), jnp.bfloat16),
            pltpu.VMEM((2, SUB, d_model), jnp.bfloat16),
            dma((2,)), dma((2, 2)), dma((2,)),
        ] + ring_scratch(up_rows, d_ff) + ring_scratch(down_rows, d_model),
        compiler_params=pltpu.CompilerParams(collective_id=0, has_side_effects=True, vmem_limit_bytes=60 * 1024 * 1024),
        cost_estimate=pl.CostEstimate(flops=4 * n_rows * d_model * d_ff, bytes_accessed=8 * d_model * d_ff, transcendentals=0),
        name="ring_ffn",
    )(owner.reshape(1), x, up, down, up_pieces, down_pieces)

    def whole(landed, way, rows, distance, own):
        first = jnp.maximum(distance - 1, 0) * way.lag * rows
        flat = landed.reshape(-1, landed.shape[-1])
        return jnp.where(owner == 1, own, lax.dynamic_slice_in_dim(flat, first, own.shape[0], 0))

    return out, lambda hot, me: (
        whole(up_landed, up_way, up_rows, (me - hot) % group, up),
        whole(down_landed, down_way, down_rows, (hot - me) % group, down))


def gelu(v):
    return jax.nn.gelu(v, approximate=True)


def ffn_in(rows, up):
    hidden = jnp.dot(rows, up, preferred_element_type=jnp.float32)
    return gelu(hidden).astype(jnp.bfloat16)


def ffn_out(hidden, down):
    out = jnp.dot(hidden, down, preferred_element_type=jnp.float32)
    return lax.reduce_precision(out, 8, 7).astype(jnp.bfloat16)


def solution(mesh):
    group = mesh.shape['expert']
    axes = tuple(mesh.axis_names)

    def local_moe(x, idx, gate, up, down):
        n_tok, d_model = x.shape
        up, down = up[0], down[0]
        n_exp = group
        me = lax.axis_index('expert')
        experts = jnp.arange(n_exp, dtype=jnp.int32)

        counts = jnp.sum((idx[:, :, None] == experts).astype(jnp.int32), axis=(0, 1))
        hot = jnp.argmax(counts).astype(jnp.int32)
        first_hot = idx[:, 0] == hot
        cold = jnp.where(first_hot, idx[:, 1], idx[:, 0])
        gate_hot = jnp.where(first_hot, gate[:, 0], gate[:, 1])[:, None]
        gate_cold = jnp.where(first_hot, gate[:, 1], gate[:, 0])[:, None]

        cold_counts = jnp.where(experts == hot, 0, counts)
        rounds = lax.pmax((jnp.max(cold_counts) + SLOTS - 1) // SLOTS, axes)
        cold, rounds = lax.optimization_barrier((cold, rounds))
        mine = (cold[:, None] == experts).astype(jnp.int32).reshape(n_tok // 128, 128, n_exp)
        lower = jnp.tril(jnp.ones((128, 128), jnp.float32), -1)
        within = jnp.einsum('ij,bje->bie', lower, mine.astype(jnp.float32)).astype(jnp.int32)
        block_sum = jnp.sum(mine, axis=1)
        before = jnp.cumsum(block_sum, axis=0) - block_sum
        rank = jnp.sum(mine * (before[:, None, :] + within), axis=-1).reshape(-1)
        def outward(r):
            here = rank - r * SLOTS
            slot = jnp.where((here >= 0) & (here < SLOTS), cold * SLOTS + here, -1)
            hit = slot[None, :] == jnp.arange(n_exp * SLOTS, dtype=jnp.int32)[:, None]
            slot_tok = jnp.sum(jnp.where(hit, jnp.arange(n_tok, dtype=jnp.int32)[None, :], 0), axis=1)
            send = x.at[slot_tok].get(mode='promise_in_bounds').reshape(n_exp, SLOTS, d_model)
            return lax.all_to_all(send, 'expert', 0, 0, tiled=True).reshape(n_exp * SLOTS, d_model)

        def homeward(r, hidden):
            out = ffn_out(hidden, down).reshape(n_exp, SLOTS, d_model)
            return lax.all_to_all(out, 'expert', 0, 0, tiled=True).reshape(n_exp * SLOTS, d_model)

        def pick(r, back):
            here = jnp.clip(rank - r * SLOTS, 0, SLOTS - 1)
            return back.at[cold * SLOTS + here].get(mode='promise_in_bounds')

        def combine(hot_out, cold_row):
            return (gate_hot * hot_out.astype(jnp.float32) + gate_cold * cold_row.astype(jnp.float32)).astype(jnp.bfloat16)

        owner = (me == hot).astype(jnp.int32)
        cold_out, gather_hot = ring_ffn(group, owner, outward(0), up, down)
        back = lax.all_to_all(cold_out.reshape(n_exp, SLOTS, d_model), 'expert', 0, 0, tiled=True).reshape(n_exp * SLOTS, d_model)
        hot_up, hot_down = gather_hot(hot, me)
        hot_hidden = ffn_in(x, hot_up)
        hot_out = ffn_out(hot_hidden, hot_down)
        hot_out, back = lax.optimization_barrier((hot_out, back))
        cold_row = pick(0, back)
        y = combine(hot_out, cold_row)

        def more(state):
            r, y = state
            new = combine(hot_out, pick(r, homeward(r, ffn_in(outward(r), up))))
            return r + 1, jnp.where((rank // SLOTS == r)[:, None], new, y)

        return lax.while_loop(lambda state: state[0] < rounds, more, (jnp.int32(1), y))[1]

    tok_spec = P(('data', 'expert'), None)
    w_spec = P('expert', None, None)
    return jax.shard_map(local_moe, mesh=mesh, in_specs=(tok_spec, tok_spec, tok_spec, w_spec, w_spec), out_specs=tok_spec, check_vma=False)
```

profile of v0, /device:TPU:112, one launch (start us, length us, event | category | flops | bytes accessed | tf_op | source)
XLA Modules:
  0.0 784.2 jit_solution(4947094835080279263)
XLA Ops:
  0.0 0.9 convert_reduce_fusion
  0.9 0.7 iota_reduce_fusion
  1.6 1.3 fusion.41
  3.5 0.8 fusion.48
  4.4 30.7 %pmax.7 = s32[]{:T(128)} all-reduce(s32[]{:T(128)S(6)} %select_n.150), channel_id=1, replica_groups=mesh['data'=2,'expert'=8] {'data','expert'}, use_global_device_ids=true, to_apply=%region_3.4 | all-reduce | flops 1 | bytes 8 | tf_op jit(solution)/shard_map/pmax | solution.py:268
  35.1 0.6 compare_select_fusion.4
  35.7 0.0 copy-start.4
  35.8 0.3 convert_reduce_fusion.1
  36.1 0.2 fusion.32
  36.4 0.0 copy-start
  36.4 0.6 fusion.40
  37.0 3.0 select_reduce_fusion.1
  40.1 32.1 %gather_fusion.2 = bf16[3584,2048]{1,0:T(8,128)(2,1)} fusion(bf16[2048,2048]{1,0:T(8,128)(2,1)} %param.7, s32[4096]{0:T(1024)S(1)} %pad_clamp_fusion.1), kind=kCustom, calls=%fused_computation.2 | custom fusion | bytes 29374464 | tf_op jit(solution)/shard_map/gather | solution.py:281
  72.2 0.0 copy-done.4
  72.2 0.0 copy-start.12
  72.2 0.0 copy-start.14
  72.2 5.9 all-to-all-start.2
  80.0 0.0 copy-done
  80.0 0.6 sign.27
  80.6 0.0 copy-done.12
  80.6 0.0 copy-done.14
  80.6 1.3 compare_select_fusion.6
  81.9 158.0 %all-to-all-done.2 = bf16[8,448,2048]{2,1,0:T(8,128)(2,1)} async-done(((bf16[8,448,2048]{2,1,0:T(8,128)(2,1)}), bf16[8,448,2048]{2,1,0:T(8,128)(2,1)}, u32[]{:S(2)}, u32[]{:S(2)}) %all-to-all-start.2) | async-done | bytes 14680096 | tf_op jit(solution)/shard_map/all_to_all | solution.py:282
  239.9 342.0 %ring_ffn.1 = (bf16[3584,2048]{1,0:T(8,128)(2,1)}, bf16[158,16,5632]{2,1,0:T(8,128)(2,1)}, bf16[112,64,2048]{2,1,0:T(8,128)(2,1)}) custom-call(s32[1]{0:T(128)} %bitcast.10.owner, bf16[3584,2048]{1,0:T(8,128)(2,1)} %bitcast.18.x_hbm, bf16[2048,5632]{1,0:T(8,128)(2,1)} %bitcast.103, bf16[5632,2048]{1,0:T(8,128)(2,1)} %bitcast.106, ...), custom_call_target="tpu_custom_call" | custom-call | flops 165356240896 | bytes 92274688 | tf_op jit(solution)/shard_map/ring_ffn/pallas_call | solution.py:205
  581.9 6.2 all-to-all-start.3
  588.1 67.8 %fusion.19 = bf16[2048,5632]{0,1:T(8,128)(2,1)} fusion(bf16[2048,2048]{1,0:T(8,128)(2,1)} %param.7, bf16[2528,5632]{1,0:T(8,128)(2,1)} %bitcast.110, s32[]{:T(128)S(6)} %select_n.156, pred[]{:T(512)S(6)} %eq.111, bf16[1,2048,5632]{2,1,0:T(8,128)(2,1)} %param.10), kind=kOutput, calls=%fused_computation.38 | convolution fusion | flops 47359983616 | bytes 77594632 | tf_op jit(solution)/shard_map/dot_general | solution.py:240
  655.9 0.0 copy-start.13
  655.9 66.3 %reduce-precision_convert_fusion.1 = bf16[2048,2048]{1,0:T(8,128)(2,1)} fusion(bf16[2048,5632]{0,1:T(8,128)(2,1)} %fusion.19, bf16[7168,2048]{1,0:T(8,128)(2,1)} %bitcast.109, s32[]{:T(128)S(6)} %select_n.160, pred[]{:T(512)S(6)} %eq.111, bf16[1,5632,2048]{2,1,0:T(8,128)(2,1)} %param.11), kind=kOutput, calls=%fused_computation.49 | convolution fusion | flops 47264563200 | bytes 77594632 | tf_op jit(solution)/shard_map/dot_general | solution.py:245
  722.2 27.4 %all-to-all-done.3 = bf16[8,448,2048]{2,1,0:T(8,128)(2,1)} async-done(((bf16[8,448,2048]{2,1,0:T(8,128)(2,1)}), bf16[8,448,2048]{2,1,0:T(8,128)(2,1)}, u32[]{:S(2)}, u32[]{:S(2)}) %all-to-all-start.3) | async-done | bytes 14680096 | tf_op jit(solution)/shard_map/all_to_all | solution.py:297
  749.6 0.0 copy-done.13
  749.6 0.0 copy-start.7
  749.6 0.0 copy-start.9
  749.6 23.4 %gather_fusion.3 = bf16[2048,2048]{1,0:T(8,128)(2,1)} fusion(bf16[3584,2048]{1,0:T(8,128)(2,1)} %bitcast.26, s32[2048]{0:T(1024)S(1)} %copy-done.13), kind=kCustom, calls=%fused_computation.3 | custom fusion | bytes 16785408 | tf_op jit(solution)/shard_map/gather | solution.py:290
  773.0 0.0 copy-start.1
  773.0 0.0 copy-start.5
  773.0 0.0 copy-done.7
  773.0 0.0 copy-done.9
  773.0 10.2 %add_convert_fusion.1 = bf16[2048,2048]{1,0:T(8,128)(2,1)} fusion(bf16[2048,2048]{1,0:T(8,128)(2,1)} %gather_fusion.3, bf16[2048,2048]{1,0:T(8,128)(2,1)} %reduce-precision_convert_fusion.1, f32[2048]{0:T(1024)S(1)} %bitcast.98, f32[2048]{0:T(1024)S(1)} %bitcast.96), kind=kLoop, calls=%fused_computation.48 | loop fusion | flops 25165824 | bytes 25182208 | tf_op jit(solution)/shard_map/convert_element_type | solution.py:293
  783.2 0.0 copy-done.1
  783.2 0.0 copy-done.5
  783.2 0.8 while.12
  (5 shorter events, 0.1 us)
Async XLA Ops:
  35.7 36.4 %copy-start.4 = (s32[2048]{0:T(1024)}, s32[2048]{0:T(1024)S(1)}, u32[]{:S(2)}) copy-start(s32[2048]{0:T(1024)S(1)} %compare_select_fusion.4) | copy-start | bytes 24580
  36.4 43.6 %copy-start = (s32[16,128]{1,0:T(8,128)}, s32[16,128]{1,0:T(8,128)S(1)}, u32[]{:S(2)}) copy-start(s32[16,128]{1,0:T(8,128)S(1)} %fusion.32) | copy-start | bytes 24580
  72.2 8.5 %copy-start.12 = (s32[2048,2]{0,1:T(2,128)S(1)}, s32[2048,2]{0,1:T(2,128)}, u32[]{:S(2)}) copy-start(s32[2048,2]{0,1:T(2,128)} %param.8) | copy-start | bytes 49156
  72.2 8.5 %copy-start.14 = (f32[2048,2]{0,1:T(2,128)S(1)}, f32[2048,2]{0,1:T(2,128)}, u32[]{:S(2)}) copy-start(f32[2048,2]{0,1:T(2,128)} %param.9) | copy-start | bytes 49156
  72.2 167.7 %all-to-all-start.2 = ((bf16[8,448,2048]{2,1,0:T(8,128)(2,1)}), bf16[8,448,2048]{2,1,0:T(8,128)(2,1)}, u32[]{:S(2)}, u32[]{:S(2)}) async-start(bf16[8,448,2048]{2,1,0:T(8,128)(2,1)} %bitcast.87), calls=%async_computation.2 | async-start | bytes 29360128 | tf_op jit(solution)/shard_map/all_to_all | solution.py:282
  581.9 167.7 %all-to-all-start.3 = ((bf16[8,448,2048]{2,1,0:T(8,128)(2,1)}), bf16[8,448,2048]{2,1,0:T(8,128)(2,1)}, u32[]{:S(2)}, u32[]{:S(2)}) async-start(bf16[8,448,2048]{2,1,0:T(8,128)(2,1)} %bitcast.88), calls=%async_computation.3 | async-start | bytes 29360128 | tf_op jit(solution)/shard_map/all_to_all | solution.py:297
  655.9 93.7 %copy-start.13 = (s32[2048]{0:T(1024)S(1)}, s32[2048]{0:T(1024)}, u32[]{:S(2)}) copy-start(s32[2048]{0:T(1024)} %get-tuple-element.197) | copy-start | bytes 24580
  749.6 23.4 %copy-start.7 = (f32[2048,1]{0,1:T(1,128)S(1)}, f32[2048,1]{0,1:T(1,128)}, u32[]{:S(2)}) copy-start(f32[2048,1]{0,1:T(1,128)} %get-tuple-element.284) | copy-start | bytes 24580
  749.6 23.4 %copy-start.9 = (f32[2048,1]{0,1:T(1,128)S(1)}, f32[2048,1]{0,1:T(1,128)}, u32[]{:S(2)}) copy-start(f32[2048,1]{0,1:T(1,128)} %get-tuple-element.286) | copy-start | bytes 24580
  773.0 10.2 %copy-start.1 = (s32[16,128]{1,0:T(8,128)S(1)}, s32[16,128]{1,0:T(8,128)}, u32[]{:S(2)}) copy-start(s32[16,128]{1,0:T(8,128)} %copy-done) | copy-start | bytes 24580
  773.0 10.2 %copy-start.5 = (s32[2048]{0:T(1024)S(1)}, s32[2048]{0:T(1024)}, u32[]{:S(2)}) copy-start(s32[2048]{0:T(1024)} %copy-done.4) | copy-start | bytes 24580
where the time goes:
time: 785 us; the launch traced here: 784 us
  Pallas kernels  342 us (44%)
  waiting for transfers between devices  185 us (24%)
  matrix products  134 us (17%)
  local copies, waits for them, and re-layouts  56.3 us (7%)
  blocking collectives  30.7 us (4%)
  other arithmetic  19.6 us (2%)
  starting transfers between devices  12.1 us (2%)
    pallas_call x1, Pallas kernels, ring_ffn(): pl.pallas_call(functools.partial(ring_ffn_kernel, group, up_way, down_way...  342 us
    all_to_all x1, waiting for transfers between devices, outward(): lax.all_to_all(send, 'expert', 0, 0, tiled=True)  158 us
    dot_general x1, matrix products, ffn_in(): hidden = jnp.dot(rows, up, preferred_element_type=jnp.float32)  67.8 us
    dot_general x1, matrix products, ffn_out(): out = jnp.dot(hidden, down, preferred_element_type=jnp.float32)  66.3 us
    gather x1, local copies, waits for them, and re-layouts, outward(): x.at[slot_tok].get(mode='promise_in_bounds').reshape(n_exp, SLOTS, d_model)  32.1 us
    pmax x1, blocking collectives, local_moe(): rounds = lax.pmax((jnp.max(cold_counts) + SLOTS - 1) // SLOTS, axes)  30.7 us
    all_to_all x1, waiting for transfers between devices, local_moe(): lax.all_to_all(cold_out.reshape(n_exp, SLOTS, d_model), 'expert', 0, 0, t...  27.4 us
    gather x1, local copies, waits for them, and re-layouts, pick(): return back.at[cold * SLOTS + here].get(mode='promise_in_bounds')  23.4 us
  transfers between devices with their start and end apart: 2, of which 2 were waited for; matrix products, arithmetic and copies ran while one was open for 17% of the time, Pallas kernels for 0%

commit v1 on v0

--- a/solution.py
+++ b/solution.py
@@ -7,20 +7,32 @@
 from jax.experimental.pallas import tpu as pltpu
 from jax.sharding import PartitionSpec as P
 
-SLOTS = 448
-SUB = 256
-SUBS = 7
-FF_STEP = 512
+SLOTS = 440
+SUB = 352
+SUBS = 5
+FF_STEP = 1408
+FF_CUTS = 0, 768, 1408
+OUT_PART = 1024
 RING = 64
+PIECE_ROWS = 16, 64
+LAGS = (5, 3), (4, 3)
+UP_TICKS = 25, 18
+TICKS = 4
 MESH = pl.DeviceIdType.MESH
 
 
 class Way:
-    def __init__(self, pieces, lag, group):
-        self.pieces, self.lag = pieces, lag
-        self.slots = pieces + (group - 2) * lag
-
-    def bind(self, owner, weights, landed, both, out, own_sem, got_sem, send_sem, recv_sem, target):
+    def __init__(self, pieces, lags, near, group):
+        self.pieces, self.lags, self.near = pieces, lags, near
+        self.slots = pieces + (group - 2) // 2 * sum(lags)
+
+    def shift(self, hot, distance):
+        relays = jnp.maximum(distance - 1, 0)
+        near = (relays + (hot % 2 != self.near)) // 2
+        return near * self.lags[1] + (relays - near) * self.lags[0]
+
+    def bind(self, me, owner, weights, landed, both, out, own_sem, got_sem, send_sem, recv_sem, target):
+        self.lag = jnp.where(me % 2 == self.near, self.lags[1], self.lags[0])
         self.owner, self.weights, self.landed, self.both, self.out = owner, weights, landed, both, out
         self.own_sem, self.got_sem, self.send_sem, self.recv_sem, self.target = own_sem, got_sem, send_sem, recv_sem, target
 
@@ -77,13 +89,15 @@
     def finish(self):
         for t in range(self.slots - 3, self.slots):
             self.remote(t).wait_send()
-        for t in range(self.slots - self.lag, self.slots):
-            self.remote(t).wait_recv()
+        for t in range(self.slots - self.lags[0], self.slots):
+            @pl.when(t >= self.slots - self.lag)
+            def _():
+                self.remote(t).wait_recv()
 
 
 def ring_ffn_kernel(group, up_way, down_way, owner, x_hbm, up_hbm, down_hbm, up_pieces, down_pieces,
                     o_hbm, up_landed, down_landed,
-                    x_buf, acc, up_buf, down_buf, o_buf, x_sem, w_sem, o_sem,
+                    x_buf, acc, up_buf, down_buf, h_buf, o_buf, x_sem, w_sem, o_sem,
                     up_both, up_out, up_own_sem, up_got_sem, up_send_sem, up_recv_sem,
                     down_both, down_out, down_own_sem, down_got_sem, down_send_sem, down_recv_sem):
     me = lax.axis_index('expert')
@@ -92,8 +106,8 @@
     for other in (left, right):
         pl.semaphore_signal(barrier, inc=1, device_id={'expert': other}, device_id_type=MESH)
     pl.semaphore_wait(barrier, 2)
-    up_way.bind(owner, up_pieces, up_landed, up_both, up_out, up_own_sem, up_got_sem, up_send_sem, up_recv_sem, right)
-    down_way.bind(owner, down_pieces, down_landed, down_both, down_out, down_own_sem, down_got_sem, down_send_sem, down_recv_sem, left)
+    up_way.bind(me, owner, up_pieces, up_landed, up_both, up_out, up_own_sem, up_got_sem, up_send_sem, up_recv_sem, right)
+    down_way.bind(me, owner, down_pieces, down_landed, down_both, down_out, down_own_sem, down_got_sem, down_send_sem, down_recv_sem, left)
 
     big = SUB * SUBS
     supers = x_hbm.shape[0] // big
@@ -111,9 +125,12 @@
     def o_copy(i):
         return pltpu.make_async_copy(o_buf.at[i % 2], o_hbm.at[pl.ds(pl.multiple_of(i * SUB, SUB), SUB)], o_sem.at[i % 2])
 
-    def compute(e):
+    def place(e):
         s, sub = e // SUBS, e % SUBS
-        p, f = s // n_ff, s % n_ff
+        return s, sub, s // n_ff, s % n_ff, pl.ds(pl.multiple_of(sub * SUB, SUB), SUB)
+
+    def compute_start(e):
+        s, sub, p, f, rows = place(e)
 
         @pl.when((sub == 0) & (f == 0))
         def _():
@@ -133,28 +150,33 @@
                 for c in w_copies(s + 1):
                     c.start()
 
-        rows = pl.ds(pl.multiple_of(sub * SUB, SUB), SUB)
-        h = jnp.dot(x_buf[p % 2, rows, :], up_buf[s % 2], preferred_element_type=jnp.float32)
-        h = gelu(h).astype(jnp.bfloat16)
-        part = jnp.dot(h, down_buf[s % 2], preferred_element_type=jnp.float32)
+    def compute_in(e, lo, hi):
+        s, sub, p, f, rows = place(e)
+        h = jnp.dot(x_buf[p % 2, rows, :], up_buf[s % 2, :, lo:hi], preferred_element_type=jnp.float32)
+        h_buf[:, lo:hi] = gelu(h).astype(jnp.bfloat16)
+
+    def compute_out(e, lo, hi):
+        s, sub, p, f, rows = place(e)
+        part = jnp.dot(h_buf[...], down_buf[s % 2, :, lo:hi], preferred_element_type=jnp.float32)
 
         @pl.when(f == 0)
         def _():
-            acc[rows, :] = part
+            acc[rows, lo:hi] = part
 
         @pl.when((f > 0) & (f < n_ff - 1))
         def _():
-            acc[rows, :] += part
+            acc[rows, lo:hi] += part
 
         @pl.when(f == n_ff - 1)
         def _():
             i = p * SUBS + sub
-
-            @pl.when(i >= 2)
-            def _():
-                o_copy(i - 2).wait()
-            o_buf[i % 2] = (acc[rows, :] + part).astype(jnp.bfloat16)
-            o_copy(i).start()
+            if lo == 0:
+                @pl.when(i >= 2)
+                def _():
+                    o_copy(i - 2).wait()
+            o_buf[i % 2, :, lo:hi] = (acc[rows, lo:hi] + part).astype(jnp.bfloat16)
+            if hi == o_buf.shape[2]:
+                o_copy(i).start()
 
     x_copy(0).start()
     for c in w_copies(0):
@@ -162,24 +184,40 @@
     up_way.load(0)
     down_way.load(0)
 
+    more, less = UP_TICKS
+
+    def tick(n):
+        @pl.when(n <= up_way.slots)
+        def _():
+            up_way.event(n)
+
+        b = n * less // more
+
+        @pl.when(((n + 1) * less // more > b) & (b <= down_way.slots))
+        def _():
+            down_way.event(b)
+
+    d_model = o_buf.shape[2]
+    work = [functools.partial(compute_in, lo=lo, hi=hi) for lo, hi in zip(FF_CUTS[:-1], FF_CUTS[1:])]
+    work += [functools.partial(compute_out, lo=lo, hi=lo + OUT_PART) for lo in range(0, d_model, OUT_PART)]
+
     def body(e, carry):
-        @pl.when(e <= up_way.slots)
-        def _():
-            up_way.event(e)
-
-        b = (e // 4) * 3 + e % 4
-
-        @pl.when((e % 4 != 3) & (b <= down_way.slots))
-        def _():
-            down_way.event(b)
-
-        @pl.when(e < steps * SUBS)
-        def _():
-            compute(e)
+        live = e < steps * SUBS
+
+        @pl.when(live)
+        def _():
+            compute_start(e)
+        for i, part in enumerate(work):
+            if i < TICKS:
+                tick(e * TICKS + i)
+
+            @pl.when(live)
+            def _():
+                part(e)
         return carry
 
-    n_events = max(steps * SUBS, up_way.slots + 1, (down_way.slots // 3 + 1) * 4)
-    lax.fori_loop(0, n_events, body, 0)
+    n_ticks = max(up_way.slots + 1, ((down_way.slots + 1) * more + less - 1) // less + 1)
+    lax.fori_loop(0, max(steps * SUBS, -(-n_ticks // TICKS)), body, 0)
     up_way.finish()
     down_way.finish()
     n_out = supers * SUBS
@@ -190,8 +228,8 @@
 def ring_ffn(group, owner, x, up, down):
     n_rows, d_model = x.shape
     d_ff = up.shape[1]
-    up_rows, down_rows = 16, 64
-    up_way, down_way = Way(d_model // up_rows, 5, group), Way(d_ff // down_rows, 4, group)
+    up_rows, down_rows = PIECE_ROWS
+    up_way, down_way = Way(d_model // up_rows, LAGS[0], 1, group), Way(d_ff // down_rows, LAGS[1], 0, group)
     up_pieces = up.reshape(d_model // up_rows, up_rows, d_ff)
     down_pieces = down.reshape(d_ff // down_rows, down_rows, d_model)
     hbm = pl.BlockSpec(memory_space=pl.ANY)
@@ -214,22 +252,23 @@
             pltpu.VMEM((big, d_model), jnp.float32),
             pltpu.VMEM((2, d_model, FF_STEP), jnp.bfloat16),
             pltpu.VMEM((2, FF_STEP, d_model), jnp.bfloat16),
+            pltpu.VMEM((SUB, FF_STEP), jnp.bfloat16),
             pltpu.VMEM((2, SUB, d_model), jnp.bfloat16),
             dma((2,)), dma((2, 2)), dma((2,)),
         ] + ring_scratch(up_rows, d_ff) + ring_scratch(down_rows, d_model),
-        compiler_params=pltpu.CompilerParams(collective_id=0, has_side_effects=True, vmem_limit_bytes=60 * 1024 * 1024),
+        compiler_params=pltpu.CompilerParams(collective_id=0, has_side_effects=True, vmem_limit_bytes=62 * 1024 * 1024),
         cost_estimate=pl.CostEstimate(flops=4 * n_rows * d_model * d_ff, bytes_accessed=8 * d_model * d_ff, transcendentals=0),
         name="ring_ffn",
     )(owner.reshape(1), x, up, down, up_pieces, down_pieces)
 
-    def whole(landed, way, rows, distance, own):
-        first = jnp.maximum(distance - 1, 0) * way.lag * rows
+    def whole(landed, way, rows, hot, distance, own):
+        first = way.shift(hot, distance) * rows
         flat = landed.reshape(-1, landed.shape[-1])
         return jnp.where(owner == 1, own, lax.dynamic_slice_in_dim(flat, first, own.shape[0], 0))
 
     return out, lambda hot, me: (
-        whole(up_landed, up_way, up_rows, (me - hot) % group, up),
-        whole(down_landed, down_way, down_rows, (hot - me) % group, down))
+        whole(up_landed, up_way, up_rows, hot, (me - hot) % group, up),
+        whole(down_landed, down_way, down_rows, hot, (hot - me) % group, down))
 
 
 def gelu(v):
@@ -266,13 +305,13 @@
 
         cold_counts = jnp.where(experts == hot, 0, counts)
         rounds = lax.pmax((jnp.max(cold_counts) + SLOTS - 1) // SLOTS, axes)
-        cold, rounds = lax.optimization_barrier((cold, rounds))
         mine = (cold[:, None] == experts).astype(jnp.int32).reshape(n_tok // 128, 128, n_exp)
         lower = jnp.tril(jnp.ones((128, 128), jnp.float32), -1)
         within = jnp.einsum('ij,bje->bie', lower, mine.astype(jnp.float32)).astype(jnp.int32)
         block_sum = jnp.sum(mine, axis=1)
         before = jnp.cumsum(block_sum, axis=0) - block_sum
         rank = jnp.sum(mine * (before[:, None, :] + within), axis=-1).reshape(-1)
+
         def outward(r):
             here = rank - r * SLOTS
             slot = jnp.where((here >= 0) & (here < SLOTS), cold * SLOTS + here, -1)
@@ -293,7 +332,8 @@
             return (gate_hot * hot_out.astype(jnp.float32) + gate_cold * cold_row.astype(jnp.float32)).astype(jnp.bfloat16)
 
         owner = (me == hot).astype(jnp.int32)
-        cold_out, gather_hot = ring_ffn(group, owner, outward(0), up, down)
+        recv, rounds = lax.optimization_barrier((outward(0), rounds))
+        cold_out, gather_hot = ring_ffn(group, owner, recv, up, down)
         back = lax.all_to_all(cold_out.reshape(n_exp, SLOTS, d_model), 'expert', 0, 0, tiled=True).reshape(n_exp * SLOTS, d_model)
         hot_up, hot_down = gather_hot(hot, me)
         hot_hidden = ffn_in(x, hot_up)

time: 785 us -> 761 us (0.969)
  waiting for transfers between devices: 185 us -> 25 us
  blocking collectives: 30.7 us -> 173 us
  Pallas kernels: 342 us -> 334 us
    all_to_all x1, waiting for transfers between devices: 158 us -> 0.01 us  [outward(): lax.all_to_all(send, 'expert', 0, 0, tiled=True)]
    pmax x1, blocking collectives: 30.7 us -> 173 us  [local_moe(): rounds = lax.pmax((jnp.max(cold_counts) + SLOTS - 1) // SLOTS, axes)]
  transfers between devices with their start and end apart: 2 -> 2, of which waited for: 2 -> 1; matrix products, arithmetic and copies ran while one was open for 17% -> 18% of each run, Pallas kernels for 0% -> 0%
where the time goes in v1:
time: 761 us
  Pallas kernels  334 us (44%)
  blocking collectives  173 us (23%)
  matrix products  134 us (18%)
  local copies, waits for them, and re-layouts  55.3 us (7%)
  waiting for transfers between devices  25 us (3%)
  other arithmetic  21.7 us (3%)
  starting transfers between devices  11.8 us (2%)
    pallas_call x1, Pallas kernels, ring_ffn(): pl.pallas_call(functools.partial(ring_ffn_kernel, group, up_way, down_way...  334 us
    pmax x1, blocking collectives, local_moe(): rounds = lax.pmax((jnp.max(cold_counts) + SLOTS - 1) // SLOTS, axes)  173 us
    dot_general x1, matrix products, ffn_in(): hidden = jnp.dot(rows, up, preferred_element_type=jnp.float32)  67.6 us
    dot_general x1, matrix products, ffn_out(): out = jnp.dot(hidden, down, preferred_element_type=jnp.float32)  66.3 us
    gather x1, local copies, waits for them, and re-layouts, outward(): x.at[slot_tok].get(mode='promise_in_bounds').reshape(n_exp, SLOTS, d_model)  32 us
    all_to_all x1, waiting for transfers between devices, local_moe(): lax.all_to_all(cold_out.reshape(n_exp, SLOTS, d_model), 'expert', 0, 0, t...  25 us
    gather x1, local copies, waits for them, and re-layouts, pick(): return back.at[cold * SLOTS + here].get(mode='promise_in_bounds')  23.3 us
  transfers between devices with their start and end apart: 2, of which 1 were waited for; matrix products, arithmetic and copies ran while one was open for 18% of the time, Pallas kernels for 0%

profile of v1, /device:TPU:112, one launch (start us, length us, event | category | flops | bytes accessed | tf_op | source)
XLA Modules:
  0.0 760.8 jit_solution(13781939973551266054)
XLA Ops:
  0.0 0.9 convert_reduce_fusion
  0.9 0.7 iota_reduce_fusion
  1.6 1.5 fusion.47
  3.1 0.3 convert_reduce_fusion.1
  3.5 0.2 fusion.32
  3.7 0.0 copy-start
  3.7 1.3 add_select_fusion.2
  5.0 2.9 select_reduce_fusion.1
  8.0 32.0 %gather_fusion.2 = bf16[3520,2048]{1,0:T(8,128)(2,1)} fusion(bf16[2048,2048]{1,0:T(8,128)(2,1)} %param.7, s32[4096]{0:T(1024)S(1)} %pad_clamp_fusion.1), kind=kCustom, calls=%fused_computation.2 | custom fusion | bytes 28849920 | tf_op jit(solution)/shard_map/gather | solution.py:320
  40.0 0.0 copy-start.9
  40.0 0.0 copy-start.11
  40.0 5.8 all-to-all-start.2
  45.8 1.3 fusion.40
  47.8 172.7 %pmax.7 = s32[]{:T(128)} all-reduce(s32[]{:T(128)S(6)} %select_n.180), channel_id=1, replica_groups=mesh['data'=2,'expert'=8] {'data','expert'}, use_global_device_ids=true, to_apply=%region_7.8 | all-reduce | flops 1 | bytes 8 | tf_op jit(solution)/shard_map/pmax | solution.py:307
  224.6 0.0 copy-done
  224.7 0.6 fusion.48
  225.3 0.6 broadcast_clamp_fusion.1
  225.9 0.0 copy-done.9
  225.9 0.0 copy-done.11
  225.9 1.3 compare_select_fusion.7
  227.2 0.0 all-to-all-done.2
  227.2 334.2 %ring_ffn.1 = (bf16[3520,2048]{1,0:T(8,128)(2,1)}, bf16[152,16,5632]{2,1,0:T(8,128)(2,1)}, bf16[109,64,2048]{2,1,0:T(8,128)(2,1)}) custom-call(s32[1]{0:T(128)} %bitcast.10.owner, bf16[3520,2048]{1,0:T(8,128)(2,1)} %bitcast.18.x_hbm, bf16[2048,5632]{1,0:T(8,128)(2,1)} %bitcast.106, bf16[5632,2048]{1,0:T(8,128)(2,1)} %bitcast.109, ...), custom_call_target="tpu_custom_call" | custom-call | flops 162403450880 | bytes 92274688 | tf_op jit(solution)/shard_map/ring_ffn/pallas_call | solution.py:243
  561.4 6.0 all-to-all-start.3
  567.4 67.6 %fusion.19 = bf16[2048,5632]{0,1:T(8,128)(2,1)} fusion(bf16[2048,2048]{1,0:T(8,128)(2,1)} %param.7, bf16[2432,5632]{1,0:T(8,128)(2,1)} %bitcast.113, s32[]{:T(128)S(6)} %select_n.184, pred[]{:T(512)S(6)} %eq.119, bf16[1,2048,5632]{2,1,0:T(8,128)(2,1)} %param.10), kind=kOutput, calls=%fused_computation.38 | convolution fusion | flops 47359983616 | bytes 77594632 | tf_op jit(solution)/shard_map/dot_general | solution.py:279
  635.0 0.0 copy-start.10
  635.0 66.3 %reduce-precision_convert_fusion.1 = bf16[2048,2048]{1,0:T(8,128)(2,1)} fusion(bf16[2048,5632]{0,1:T(8,128)(2,1)} %fusion.19, bf16[6976,2048]{1,0:T(8,128)(2,1)} %bitcast.112, s32[]{:T(128)S(6)} %select_n.189, pred[]{:T(512)S(6)} %eq.119, bf16[1,5632,2048]{2,1,0:T(8,128)(2,1)} %param.11), kind=kOutput, calls=%fused_computation.49 | convolution fusion | flops 47264563200 | bytes 77594632 | tf_op jit(solution)/shard_map/dot_general | solution.py:284
  701.3 25.0 %all-to-all-done.3 = bf16[8,440,2048]{2,1,0:T(8,128)(2,1)} async-done(((bf16[8,440,2048]{2,1,0:T(8,128)(2,1)}), bf16[8,440,2048]{2,1,0:T(8,128)(2,1)}, u32[]{:S(2)}, u32[]{:S(2)}) %all-to-all-start.3) | async-done | bytes 14417952 | tf_op jit(solution)/shard_map/all_to_all | solution.py:337
  726.4 0.0 copy-done.10
  726.4 0.0 copy-start.4
  726.4 0.0 copy-start.6
  726.4 23.3 %gather_fusion.3 = bf16[2048,2048]{1,0:T(8,128)(2,1)} fusion(bf16[3520,2048]{1,0:T(8,128)(2,1)} %bitcast.26, s32[2048]{0:T(1024)S(1)} %copy-done.10), kind=kCustom, calls=%fused_computation.3 | custom fusion | bytes 16785408 | tf_op jit(solution)/shard_map/gather | solution.py:329
  749.7 0.0 copy-start.1
  749.7 0.0 copy-done.4
  749.7 0.0 copy-done.6
  749.7 10.2 %add_convert_fusion.1 = bf16[2048,2048]{1,0:T(8,128)(2,1)} fusion(bf16[2048,2048]{1,0:T(8,128)(2,1)} %gather_fusion.3, bf16[2048,2048]{1,0:T(8,128)(2,1)} %reduce-precision_convert_fusion.1, f32[2048]{0:T(1024)S(1)} %bitcast.97, f32[2048]{0:T(1024)S(1)} %bitcast.95), kind=kLoop, calls=%fused_computation.48 | loop fusion | flops 25165824 | bytes 25182208 | tf_op jit(solution)/shard_map/convert_element_type | solution.py:332
  759.9 0.0 copy-done.1
  759.9 0.7 while.12
  (6 shorter events, 0.1 us)
Async XLA Ops:
  3.7 220.9 %copy-start = (s32[16,128]{1,0:T(8,128)}, s32[16,128]{1,0:T(8,128)S(1)}, u32[]{:S(2)}) copy-start(s32[16,128]{1,0:T(8,128)S(1)} %fusion.32) | copy-start | bytes 24580
  40.0 185.9 %copy-start.9 = (s32[2048,2]{0,1:T(2,128)S(1)}, s32[2048,2]{0,1:T(2,128)}, u32[]{:S(2)}) copy-start(s32[2048,2]{0,1:T(2,128)} %param.8) | copy-start | bytes 49156
  40.0 185.9 %copy-start.11 = (f32[2048,2]{0,1:T(2,128)S(1)}, f32[2048,2]{0,1:T(2,128)}, u32[]{:S(2)}) copy-start(f32[2048,2]{0,1:T(2,128)} %param.9) | copy-start | bytes 49156
  40.0 187.1 %all-to-all-start.2 = ((bf16[8,440,2048]{2,1,0:T(8,128)(2,1)}), bf16[8,440,2048]{2,1,0:T(8,128)(2,1)}, u32[]{:S(2)}, u32[]{:S(2)}) async-start(bf16[8,440,2048]{2,1,0:T(8,128)(2,1)} %bitcast.88), calls=%async_computation.2 | async-start | bytes 28835840 | tf_op jit(solution)/shard_map/all_to_all | solution.py:321
  561.4 165.0 %all-to-all-start.3 = ((bf16[8,440,2048]{2,1,0:T(8,128)(2,1)}), bf16[8,440,2048]{2,1,0:T(8,128)(2,1)}, u32[]{:S(2)}, u32[]{:S(2)}) async-start(bf16[8,440,2048]{2,1,0:T(8,128)(2,1)} %bitcast.89), calls=%async_computation.3 | async-start | bytes 28835840 | tf_op jit(solution)/shard_map/all_to_all | solution.py:337
  635.0 91.4 %copy-start.10 = (s32[2048]{0:T(1024)S(1)}, s32[2048]{0:T(1024)}, u32[]{:S(2)}) copy-start(s32[2048]{0:T(1024)} %broadcast_clamp_fusion.1) | copy-start | bytes 24580
  726.4 23.3 %copy-start.4 = (f32[2048,1]{0,1:T(1,128)S(1)}, f32[2048,1]{0,1:T(1,128)}, u32[]{:S(2)}) copy-start(f32[2048,1]{0,1:T(1,128)} %get-tuple-element.287) | copy-start | bytes 24580
  726.4 23.3 %copy-start.6 = (f32[2048,1]{0,1:T(1,128)S(1)}, f32[2048,1]{0,1:T(1,128)}, u32[]{:S(2)}) copy-start(f32[2048,1]{0,1:T(1,128)} %get-tuple-element.289) | copy-start | bytes 24580
  749.7 10.2 %copy-start.1 = (s32[16,128]{1,0:T(8,128)S(1)}, s32[16,128]{1,0:T(8,128)}, u32[]{:S(2)}) copy-start(s32[16,128]{1,0:T(8,128)} %copy-done) | copy-start | bytes 24580
